TPU v7x, 32 devices: a whole 2x2x4 slice. The times are simulated.
32 devices in a mesh: row: 16 (over z, x, core), chan: 2 (over y).
Axes of the slice: x: 2, y: 2, z: 4, core: 2. Of those that a mesh axis runs over, the one named last changes fastest.
Arguments:
- pair_rep: float32 [256, 256, 128], P('row', 'chan'), may hold values from -630 to 630
- residue_mask: int32 [256], replicated, may hold values from 0 to 1, as said below
- norm_gain: float32 [128], replicated, may hold values from 0.5 to 1.5
- norm_shift: float32 [128], replicated, may hold values from -3 to 3
- proj_weight: float32 [128, 512], replicated, may hold values from -4 to 4
- gate_shift: float32 [128], replicated, may hold values from -4 to 4
- bias_weight: float32 [128, 4], replicated, may hold values from -0.5 to 0.5
- out_weight: float32 [128, 128], replicated, may hold values from -0.5 to 0.5
Outputs:
- update: float32 [256, 256, 128], P('row', 'chan')
Inputs may be any that keep to these rules, and one draw needn't show every extreme that they name: `residue_mask`: residue 0 is always valid.
All inputs are finite; a program needn't handle non-finite values.
Results may differ from a plain program's by a relative error of at most 0.012.
Values may be sent and summed in bfloat16 or wider, within the bound.
No kernel may reach another device: no remote copies, remote signals or barrier semaphores. Data moves between devices by JAX's collectives and lax.ppermute only.
A program may use at most 64 MiB of HBM per device.

v0:
```python
import math
import jax
import jax.numpy as jnp
from jax import lax
from jax.sharding import PartitionSpec as P

C = 128
HEADS = 4


def normalize(values, norm_gain, norm_shift):
    average = jnp.mean(values, axis=-1, keepdims=True)
    centered = values - average
    variance = jnp.mean(centered * centered, axis=-1, keepdims=True)
    return centered * lax.rsqrt(variance + 1e-05) * norm_gain + norm_shift


def body(
    pair_rep, residue_mask, norm_gain, norm_shift, proj_weight, gate_shift, bias_weight, out_weight
):
    highest = lax.Precision.HIGHEST
    head_dim = C // HEADS
    scaling = 1.0 / math.sqrt(head_dim)
    pair_rows, span, width = pair_rep.shape
    normed = normalize(pair_rep, norm_gain, norm_shift)
    projected = jnp.einsum("rjc,ce->rje", normed, proj_weight, precision=highest)
    query_half = (
        (projected[:, :, :width] * scaling)
        .astype(jnp.bfloat16)
        .reshape(pair_rows, span, HEADS, head_dim)
    )
    key_half = projected[:, :, width : 2 * width].astype(jnp.bfloat16)
    value_half = projected[:, :, 2 * width : 3 * width].astype(jnp.bfloat16)
    gates = projected[:, :, 3 * width :]
    bias_local = jnp.einsum("rjc,ch->hrj", normed, bias_weight, precision=highest)
    bias_cols = lax.all_gather(bias_local, "row", axis=1, tiled=True)
    own_bias = lax.all_to_all(bias_cols, "chan", split_axis=1, concat_axis=2, tiled=True)
    valid_keys = residue_mask > 0
    key_all, value_all = (
        lax.all_gather(key_half, "chan", axis=1, tiled=True),
        lax.all_gather(value_half, "chan", axis=1, tiled=True),
    )

    def one_row(operands):
        queries, key_row, value_row = operands
        key_heads = key_row.reshape(-1, HEADS, head_dim)
        scores = (
            jnp.einsum("jhd,khd->hjk", queries, key_heads, preferred_element_type=jnp.float32)
            + own_bias
        )
        weights = jax.nn.softmax(
            jnp.where(valid_keys[None, None, :], scores, -1000000000.0), axis=-1
        )
        values = value_row.astype(jnp.float32).reshape(-1, HEADS, head_dim)
        return jnp.einsum("hjk,khd->jhd", weights, values, precision=highest)

    attended = lax.map(one_row, (query_half, key_all, value_all)).reshape(pair_rows, span, width)
    gated_rows = jax.nn.sigmoid(gates + gate_shift) * attended
    return jnp.einsum("rjd,dc->rjc", gated_rows, out_weight, precision=highest)


def solution(mesh):
    return jax.shard_map(
        body,
        mesh=mesh,
        in_specs=(P("row", "chan", None), P(), P(), P(), P(), P(), P(), P()),
        out_specs=P("row", "chan", None),
        check_vma=False,
    )
```

profile of v0, /device:TPU:0, one launch (start us, length us, event | category | flops | bytes accessed | tf_op | source)
XLA Modules:
  0.0 117.3 jit_solution(9026340137136260485)
XLA Ops:
  6.5 1.6 %reduce_sum.27 = f32[16,128]{1,0:T(8,128)S(1)} reduce(f32[16,128,128]{2,1,0:T(8,128)} %param.10, f32[]{:T(128)} %constant.8.clone.1), dimensions={2}, to_apply=%region_0.0 | reduce | flops 260096 | bytes 1056772 | tf_op jit(solution)/shard_map/reduce_sum | solution.py:12
  8.2 1.9 %multiply_reduce_fusion = f32[16,128]{1,0:T(8,128)S(1)} fusion(f32[16,128,128]{2,1,0:T(8,128)} %param.10, f32[16,128]{1,0:T(8,128)S(1)} %broadcast_multiply_fusion), kind=kLoop, calls=%fused_computation.24 | loop fusion | flops 784384 | bytes 1064960 | tf_op jit(solution)/shard_map/reduce_sum | solution.py:14
  10.1 6.7 %fusion.34 = (bf16[16,128,512]{2,1,0:T(8,128)(2,1)S(1)}, f32[16,128,512]{2,1,0:T(8,128)}) fusion(f32[128,512]{1,0:T(8,128)S(1)} %copy-done, f32[16,128,128]{2,1,0:T(8,128)} %param.10, f32[128]{0:T(128)} %param.13, f32[128]{0:T(128)} %param.12, f32[16,128]{1,0:T(8,128)S(1)} %add_rsqrt_fusion, f32[16,128]{1,0:T(8,128)S(1)} %broadcast_multiply_fusion), kind=kOutput, calls=%fused_computation.46 | convolution fusion | flops 1612709888 | bytes 7619584 | tf_op jit(solution)/shard_map/rjc,ce->rje/dot_general | solution.py:26
  16.9 1.3 %fusion.33 = (bf16[16,128,128]{2,1,0:T(8,128)(2,1)}, bf16[16,128,128]{2,1,0:T(8,128)(2,1)}) fusion(bf16[16,128,512]{2,1,0:T(8,128)(2,1)S(1)} %get-tuple-element.84), kind=kLoop, calls=%fused_computation.45 | loop fusion | bytes 2097152 | tf_op jit(solution)/shard_map/slice | solution.py:32
  18.2 0.7 all-gather.5.cloned.1.call-update
  19.0 1.6 %convolution_bitcast_fusion.1 = f32[4,16,128]{2,0,1:T(4,128)S(1)} fusion(f32[16,128,128]{2,1,0:T(8,128)S(1)} %copy-done.1, f32[128]{0:T(128)S(1)} %copy-done.2, f32[128]{0:T(128)S(1)} %copy-done.3, f32[16,128]{1,0:T(8,128)S(1)} %add_rsqrt_fusion, f32[16,128]{1,0:T(8,128)S(1)} %broadcast_multiply_fusion, f32[128,4]{0,1:T(4,128)S(1)} %copy-done.4), kind=kOutput, calls=%fused_computation.14 | convolution fusion | flops 13631488 | bytes 1100800 | tf_op jit(solution)/shard_map/rjc,ch->hrj/dot_general | solution.py:35
  20.6 26.0 %all_gather.11 = f32[4,256,128]{2,0,1:T(4,128)} all-gather(f32[4,16,128]{2,0,1:T(4,128)S(1)} %convolution_bitcast_fusion.1), channel_id=1, replica_groups=mesh['row'=16,'chan'=2] {'row'}, dimensions={1}, use_global_device_ids=true | all-gather | bytes 557056 | tf_op jit(solution)/shard_map/all_gather | solution.py:36
  46.5 3.5 %all-to-all-start = ((f32[4,256,128]{2,0,1:T(4,128)}), f32[4,256,128]{2,0,1:T(4,128)S(1)}, u32[]{:S(2)}, u32[]{:S(2)}) async-start(f32[4,256,128]{2,0,1:T(4,128)} %all_gather.11), calls=%async_computation | async-start | bytes 1048576 | tf_op jit(solution)/shard_map/all_to_all | solution.py:37
  50.0 1.4 %fusion.9 = bf16[16,128,128]{2,1,0:T(8,128)(2,1)S(1)} fusion(f32[16,128,512]{2,1,0:T(8,128)} %get-tuple-element.85), kind=kLoop, calls=%fused_computation.16 | loop fusion | flops 524288 | bytes 1572864 | tf_op jit(solution)/shard_map/convert_element_type | solution.py:29
  51.8 12.5 %all-to-all-done = f32[4,256,128]{2,0,1:T(4,128)S(1)} async-done(((f32[4,256,128]{2,0,1:T(4,128)}), f32[4,256,128]{2,0,1:T(4,128)S(1)}, u32[]{:S(2)}, u32[]{:S(2)}) %all-to-all-start) | async-done | bytes 524320 | tf_op jit(solution)/shard_map/all_to_all | solution.py:37
  64.3 0.4 copy.20
  64.8 0.4 all_to_all.16
  65.2 5.1 %all-gather.5.cloned.1.call-done = bf16[16,256,128]{2,1,0:T(8,128)(2,1)} async-done(((bf16[16,128,128]{2,1,0:T(8,128)(2,1)}), bf16[16,256,128]{2,1,0:T(8,128)(2,1)}) %all-gather.5.cloned.1.call-update) | async-done | bytes 1048592 | tf_op jit(solution)/shard_map/all_gather | solution.py:40
  70.3 36.5 %while.10 = (s32[]{:T(128)}, f32[16,128,4,32]{1,3,2,0:T(8,128)S(1)}, bf16[16,256,128]{2,1,0:T(8,128)(2,1)}, pred[256]{0:T(512)(128)(4,1)S(1)}, bf16[16,128,4,32]...) while((s32[]{:T(128)}, ...), condition=%wide.region_5.6_spmd, body=%wide.region_2.5_spmd.sunk | while | flops 59636736 | bytes 2861665 | solution.py:57
  70.3 0.9 constant_dynamic-slice_fusion.3
  72.0 0.5 fusion.48
  72.6 0.9 constant_dynamic-slice_fusion.3
  74.3 0.5 fusion.48
  74.9 0.9 constant_dynamic-slice_fusion.3
  75.9 0.4 fusion.46
  76.6 0.5 fusion.48
  77.1 0.9 constant_dynamic-slice_fusion.3
  78.9 0.5 fusion.48
  79.4 0.9 constant_dynamic-slice_fusion.3
  81.2 0.5 fusion.48
  81.7 0.9 constant_dynamic-slice_fusion.3
  83.4 0.5 fusion.48
  84.0 0.9 constant_dynamic-slice_fusion.3
  85.7 0.5 fusion.48
  86.2 0.9 constant_dynamic-slice_fusion.3
  88.0 0.5 fusion.48
  88.5 0.9 constant_dynamic-slice_fusion.3
  90.3 0.5 fusion.48
  90.8 0.9 constant_dynamic-slice_fusion.3
  92.5 0.5 fusion.48
  93.1 0.9 constant_dynamic-slice_fusion.3
  94.8 0.5 fusion.48
  95.4 0.9 constant_dynamic-slice_fusion.3
  97.1 0.5 fusion.48
  97.6 0.9 constant_dynamic-slice_fusion.3
  99.4 0.5 fusion.48
  99.9 0.9 constant_dynamic-slice_fusion.3
  101.7 0.5 fusion.48
  102.2 0.9 constant_dynamic-slice_fusion.3
  103.9 0.5 fusion.48
  104.5 0.9 constant_dynamic-slice_fusion.3
  106.2 0.5 fusion.48
  107.1 3.3 %fusion.15 = f32[16,128,128]{2,1,0:T(8,128)} fusion(f32[16,128,128]{2,1,0:T(8,128)S(1)} %copy.23, f32[16,128,512]{2,1,0:T(8,128)} %get-tuple-element.85, f32[128]{0:T(128)S(1)} %copy-done.7, f32[128,128]{1,0:T(8,128)S(1)} %copy-done.5), kind=kOutput, calls=%fused_computation.25 | convolution fusion | flops 403963904 | bytes 3211776 | tf_op jit(solution)/shard_map/rjd,dc->rjc/dot_general | solution.py:59
  (89 shorter events, 13.8 us)
Async XLA Ops:
  6.5 3.5 %copy-start = (f32[128,512]{1,0:T(8,128)S(1)}, f32[128,512]{1,0:T(8,128)}, u32[]{:S(2)}) copy-start(f32[128,512]{1,0:T(8,128)} %param.14) | copy-start | bytes 786436
  6.5 58.7 %all-gather.3.cloned.1.call-start = ((), (), s32[]{:S(2)}) async-start(), calls=%async_computation.1 | async-start | bytes 1572864 | tf_op jit(solution)/shard_map/all_gather | solution.py:41
  10.1 8.9 %copy-start.1 = (f32[16,128,128]{2,1,0:T(8,128)S(1)}, f32[16,128,128]{2,1,0:T(8,128)}, u32[]{:S(2)}) copy-start(f32[16,128,128]{2,1,0:T(8,128)} %param.10) | copy-start | bytes 3145732
  10.1 8.9 %copy-start.2 = (f32[128]{0:T(128)S(1)}, f32[128]{0:T(128)}, u32[]{:S(2)}) copy-start(f32[128]{0:T(128)} %param.13) | copy-start | bytes 1540
  10.1 8.9 %copy-start.3 = (f32[128]{0:T(128)S(1)}, f32[128]{0:T(128)}, u32[]{:S(2)}) copy-start(f32[128]{0:T(128)} %param.12) | copy-start | bytes 1540
  10.1 8.9 %copy-start.4 = (f32[128,4]{0,1:T(4,128)S(1)}, f32[128,4]{0,1:T(4,128)}, u32[]{:S(2)}) copy-start(f32[128,4]{0,1:T(4,128)} %param.16) | copy-start | bytes 6148
  16.9 34.9 %copy-start.6 = (s32[256]{0:T(256)S(1)}, s32[256]{0:T(256)}, u32[]{:S(2)}) copy-start(s32[256]{0:T(256)} %param.11) | copy-start | bytes 3076
  18.2 52.1 %all-gather.5.cloned.1.call-start = ((), (), s32[]{:S(2)}) async-start(), calls=%async_computation.2 | async-start | bytes 1572864 | tf_op jit(solution)/shard_map/all_gather | solution.py:40
  46.5 17.8 %all-to-all-start = ((f32[4,256,128]{2,0,1:T(4,128)}), f32[4,256,128]{2,0,1:T(4,128)S(1)}, u32[]{:S(2)}, u32[]{:S(2)}) async-start(f32[4,256,128]{2,0,1:T(4,128)} %all_gather.11), calls=%async_computation | async-start | bytes 1048576 | tf_op jit(solution)/shard_map/all_to_all | solution.py:37
  70.3 36.8 %copy-start.5 = (f32[128,128]{1,0:T(8,128)S(1)}, f32[128,128]{1,0:T(8,128)}, u32[]{:S(2)}) copy-start(f32[128,128]{1,0:T(8,128)} %param.17) | copy-start | bytes 196612
  70.3 36.8 %copy-start.7 = (f32[128]{0:T(128)S(1)}, f32[128]{0:T(128)}, u32[]{:S(2)}) copy-start(f32[128]{0:T(128)} %param.15) | copy-start | bytes 1540
Sparse Core Ops, SparseCore 0:
  18.3 23.9 all-gather.2
  43.9 26.3 all-gather.4
where the time goes:
time: 118 us; the launch traced here: 117 us
  blocking collectives  26 us (22%)
  matrix products  25.9 us (22%)
  local copies, waits for them, and re-layouts  20.5 us (17%)
  waiting for transfers between devices  18.3 us (16%)
  between operations  13.6 us (12%)
  other arithmetic  9.11 us (8%)
  starting transfers between devices  3.53 us (3%)
    all_gather x1, blocking collectives, body(): bias_cols = lax.all_gather(bias_local, 'row', axis=1, tiled=True)  26 us
    dynamic_slice x48, local copies, waits for them, and re-layouts, body(): lax.map(one_row, (query_half, key_all, value_all))  17.7 us
    all_to_all x1, waiting for transfers between devices, body(): lax.all_to_all(bias_cols, 'chan', split_axis=1, concat_axis=2, tiled=True)  12.5 us
    dot_general x16, matrix products, one_row(): return jnp.einsum('hjk,khd->jhd', weights, values, precision=highest)  8.53 us
    dot_general x1, matrix products, body(): jnp.einsum('rjc,ce->rje', normed, proj_weight, precision=highest)  6.75 us
    dot_general x16, matrix products, one_row(): jnp.einsum('jhd,khd->hjk', queries, key_heads, preferred_element_type=jnp...  5.72 us
    all_gather x1, waiting for transfers between devices, body(): lax.all_gather(key_half, 'chan', axis=1, tiled=True)  5.06 us
    reduce_sum x16, other arithmetic, one_row(): jax.nn.softmax(jnp.where(valid_keys[None, None, :], scores, -1000000000.0...  4.19 us
  transfers between devices with their start and end apart: 3, of which 2 were waited for; matrix products, arithmetic and copies ran while one was open for 3% of the time, Pallas kernels for 0%

commit v1 on v0

--- a/solution.py
+++ b/solution.py
@@ -33,7 +33,12 @@
     value_half = projected[:, :, 2 * width : 3 * width].astype(jnp.bfloat16)
     gates = projected[:, :, 3 * width :]
     bias_local = jnp.einsum("rjc,ch->hrj", normed, bias_weight, precision=highest)
-    bias_cols = lax.all_gather(bias_local, "row", axis=1, tiled=True)
+    ring = [bias_local]
+    for hop in range(15):
+        ring.append(lax.ppermute(ring[-1], "row", [(dev, (dev + 1) % 16) for dev in range(16)]))
+    bias_cols = jnp.roll(
+        jnp.concatenate(ring[::-1], axis=1), (lax.axis_index("row") + 1) * ring[0].shape[1], axis=1
+    )
     own_bias = lax.all_to_all(bias_cols, "chan", split_axis=1, concat_axis=2, tiled=True)
     valid_keys = residue_mask > 0
     key_all, value_all = (

time: 118 us -> 180 us (1.53)
  waiting for transfers between devices: 18.3 us -> 104 us
  blocking collectives: 26 us -> 0 us
    ppermute x0 -> x15, waiting for transfers between devices: none -> 91 us  [body(): lax.ppermute(ring[-1], 'row', [(dev, (dev + 1) % 16) for dev in range(16)])]
    all_gather x1 -> x0, blocking collectives: 26 us -> none  [body(): bias_cols = lax.all_gather(bias_local, 'row', axis=1, tiled=True)]
    all_gather x1, waiting for transfers between devices: 5.06 us -> 2.11 us  [body(): lax.all_gather(key_half, 'chan', axis=1, tiled=True)]
    all_to_all x1, waiting for transfers between devices: 12.5 us -> 10.6 us  [body(): lax.all_to_all(bias_cols, 'chan', split_axis=1, concat_axis=2, tiled=True)]
  transfers between devices with their start and end apart: 3 -> 18, of which waited for: 2 -> 17; matrix products, arithmetic and copies ran while one was open for 3% -> 3% of each run, Pallas kernels for 0% -> 0%
where the time goes in v1:
time: 180 us; the launch traced here: 179 us
  waiting for transfers between devices  104 us (58%)
  matrix products  25.9 us (14%)
  local copies, waits for them, and re-layouts  21.6 us (12%)
  between operations  13.8 us (8%)
  other arithmetic  9.03 us (5%)
  starting transfers between devices  4.13 us (2%)
    ppermute x15, waiting for transfers between devices, body(): lax.ppermute(ring[-1], 'row', [(dev, (dev + 1) % 16) for dev in range(16)])  91 us
    dynamic_slice x48, local copies, waits for them, and re-layouts, body(): lax.map(one_row, (query_half, key_all, value_all))  17.7 us
    all_to_all x1, waiting for transfers between devices, body(): lax.all_to_all(bias_cols, 'chan', split_axis=1, concat_axis=2, tiled=True)  10.6 us
    dot_general x16, matrix products, one_row(): return jnp.einsum('hjk,khd->jhd', weights, values, precision=highest)  8.53 us
    dot_general x1, matrix products, body(): jnp.einsum('rjc,ce->rje', normed, proj_weight, precision=highest)  6.75 us
    dot_general x16, matrix products, one_row(): jnp.einsum('jhd,khd->hjk', queries, key_heads, preferred_element_type=jnp...  5.72 us
    reduce_sum x16, other arithmetic, one_row(): jax.nn.softmax(jnp.where(valid_keys[None, None, :], scores, -1000000000.0...  4.19 us
  transfers between devices with their start and end apart: 18, of which 17 were waited for; matrix products, arithmetic and copies ran while one was open for 3% of the time, Pallas kernels for 0%

profile of v1, /device:TPU:0, one launch (start us, length us, event | category | flops | bytes accessed | tf_op | source)
XLA Modules:
  0.0 178.6 jit_solution(12776692112356560990)
XLA Ops:
  6.5 1.6 reduce_sum.27
  8.2 1.9 %multiply_reduce_fusion = f32[16,128]{1,0:T(8,128)S(1)} fusion(f32[16,128,128]{2,1,0:T(8,128)} %param.10, f32[16,128]{1,0:T(8,128)S(1)} %broadcast_multiply_fusion), kind=kLoop, calls=%fused_computation.24 | loop fusion | flops 784384 | bytes 1064960 | tf_op jit(solution)/shard_map/reduce_sum | solution.py:14
  10.1 6.7 %fusion.34 = (bf16[16,128,512]{2,1,0:T(8,128)(2,1)S(1)}, f32[16,128,512]{2,1,0:T(8,128)}) fusion(f32[128,512]{1,0:T(8,128)S(1)} %copy-done, f32[16,128,128]{2,1,0:T(8,128)} %param.10, f32[128]{0:T(128)} %param.13, f32[128]{0:T(128)} %param.12, f32[16,128]{1,0:T(8,128)S(1)} %add_rsqrt_fusion, f32[16,128]{1,0:T(8,128)S(1)} %broadcast_multiply_fusion), kind=kOutput, calls=%fused_computation.79 | convolution fusion | flops 1612709888 | bytes 7619584 | tf_op jit(solution)/shard_map/rjc,ce->rje/dot_general | solution.py:26
  16.9 1.3 fusion.33
  18.2 1.6 convolution_bitcast_fusion.1
  19.9 0.5 collective-permute-start
  20.4 6.6 %collective-permute-done = f32[4,16,128]{2,0,1:T(4,128)S(1)} collective-permute-done((f32[4,16,128]{2,0,1:T(4,128)S(1)}, f32[4,16,128]{2,0,1:T(4,128)S(1)}, u32[]{:S(2)}, u32[]{:S(2)}) %collective-permute-start) | collective-permute-done | bytes 32800 | tf_op jit(solution)/shard_map/ppermute | solution.py:38
  26.9 6.0 %collective-permute-done.1 = f32[4,16,128]{2,0,1:T(4,128)S(1)} collective-permute-done((f32[4,16,128]{2,0,1:T(4,128)S(1)}, f32[4,16,128]{2,0,1:T(4,128)S(1)}, u32[]{:S(2)}, u32[]{:S(2)}) %collective-permute-start.1) | collective-permute-done | bytes 32800 | tf_op jit(solution)/shard_map/ppermute | solution.py:38
  33.0 6.0 %collective-permute-done.2 = f32[4,16,128]{2,0,1:T(4,128)S(1)} collective-permute-done((f32[4,16,128]{2,0,1:T(4,128)S(1)}, f32[4,16,128]{2,0,1:T(4,128)S(1)}, u32[]{:S(2)}, u32[]{:S(2)}) %collective-permute-start.2) | collective-permute-done | bytes 32800 | tf_op jit(solution)/shard_map/ppermute | solution.py:38
  39.0 6.0 %collective-permute-done.3 = f32[4,16,128]{2,0,1:T(4,128)S(1)} collective-permute-done((f32[4,16,128]{2,0,1:T(4,128)S(1)}, f32[4,16,128]{2,0,1:T(4,128)S(1)}, u32[]{:S(2)}, u32[]{:S(2)}) %collective-permute-start.3) | collective-permute-done | bytes 32800 | tf_op jit(solution)/shard_map/ppermute | solution.py:38
  45.1 6.0 %collective-permute-done.4 = f32[4,16,128]{2,0,1:T(4,128)S(1)} collective-permute-done((f32[4,16,128]{2,0,1:T(4,128)S(1)}, f32[4,16,128]{2,0,1:T(4,128)S(1)}, u32[]{:S(2)}, u32[]{:S(2)}) %collective-permute-start.4) | collective-permute-done | bytes 32800 | tf_op jit(solution)/shard_map/ppermute | solution.py:38
  51.1 6.0 %collective-permute-done.5 = f32[4,16,128]{2,0,1:T(4,128)S(1)} collective-permute-done((f32[4,16,128]{2,0,1:T(4,128)S(1)}, f32[4,16,128]{2,0,1:T(4,128)S(1)}, u32[]{:S(2)}, u32[]{:S(2)}) %collective-permute-start.5) | collective-permute-done | bytes 32800 | tf_op jit(solution)/shard_map/ppermute | solution.py:38
  57.1 6.0 %collective-permute-done.6 = f32[4,16,128]{2,0,1:T(4,128)S(1)} collective-permute-done((f32[4,16,128]{2,0,1:T(4,128)S(1)}, f32[4,16,128]{2,0,1:T(4,128)S(1)}, u32[]{:S(2)}, u32[]{:S(2)}) %collective-permute-start.6) | collective-permute-done | bytes 32800 | tf_op jit(solution)/shard_map/ppermute | solution.py:38
  63.2 6.0 %collective-permute-done.7 = f32[4,16,128]{2,0,1:T(4,128)S(1)} collective-permute-done((f32[4,16,128]{2,0,1:T(4,128)S(1)}, f32[4,16,128]{2,0,1:T(4,128)S(1)}, u32[]{:S(2)}, u32[]{:S(2)}) %collective-permute-start.7) | collective-permute-done | bytes 32800 | tf_op jit(solution)/shard_map/ppermute | solution.py:38
  69.2 6.0 %collective-permute-done.8 = f32[4,16,128]{2,0,1:T(4,128)S(1)} collective-permute-done((f32[4,16,128]{2,0,1:T(4,128)S(1)}, f32[4,16,128]{2,0,1:T(4,128)S(1)}, u32[]{:S(2)}, u32[]{:S(2)}) %collective-permute-start.8) | collective-permute-done | bytes 32800 | tf_op jit(solution)/shard_map/ppermute | solution.py:38
  75.2 6.0 %collective-permute-done.9 = f32[4,16,128]{2,0,1:T(4,128)S(1)} collective-permute-done((f32[4,16,128]{2,0,1:T(4,128)S(1)}, f32[4,16,128]{2,0,1:T(4,128)S(1)}, u32[]{:S(2)}, u32[]{:S(2)}) %collective-permute-start.9) | collective-permute-done | bytes 32800 | tf_op jit(solution)/shard_map/ppermute | solution.py:38
  81.3 6.0 %collective-permute-done.10 = f32[4,16,128]{2,0,1:T(4,128)S(1)} collective-permute-done((f32[4,16,128]{2,0,1:T(4,128)S(1)}, f32[4,16,128]{2,0,1:T(4,128)S(1)}, u32[]{:S(2)}, u32[]{:S(2)}) %collective-permute-start.10) | collective-permute-done | bytes 32800 | tf_op jit(solution)/shard_map/ppermute | solution.py:38
  87.3 6.0 %collective-permute-done.11 = f32[4,16,128]{2,0,1:T(4,128)S(1)} collective-permute-done((f32[4,16,128]{2,0,1:T(4,128)S(1)}, f32[4,16,128]{2,0,1:T(4,128)S(1)}, u32[]{:S(2)}, u32[]{:S(2)}) %collective-permute-start.11) | collective-permute-done | bytes 32800 | tf_op jit(solution)/shard_map/ppermute | solution.py:38
  93.4 6.0 %collective-permute-done.12 = f32[4,16,128]{2,0,1:T(4,128)S(1)} collective-permute-done((f32[4,16,128]{2,0,1:T(4,128)S(1)}, f32[4,16,128]{2,0,1:T(4,128)S(1)}, u32[]{:S(2)}, u32[]{:S(2)}) %collective-permute-start.12) | collective-permute-done | bytes 32800 | tf_op jit(solution)/shard_map/ppermute | solution.py:38
  99.4 6.0 %collective-permute-done.13 = f32[4,16,128]{2,0,1:T(4,128)S(1)} collective-permute-done((f32[4,16,128]{2,0,1:T(4,128)S(1)}, f32[4,16,128]{2,0,1:T(4,128)S(1)}, u32[]{:S(2)}, u32[]{:S(2)}) %collective-permute-start.13) | collective-permute-done | bytes 32800 | tf_op jit(solution)/shard_map/ppermute | solution.py:38
  105.5 6.0 %collective-permute-done.14 = f32[4,16,128]{2,0,1:T(4,128)S(1)} collective-permute-done((f32[4,16,128]{2,0,1:T(4,128)S(1)}, f32[4,16,128]{2,0,1:T(4,128)S(1)}, u32[]{:S(2)}, u32[]{:S(2)}) %collective-permute-start.14) | collective-permute-done | bytes 32800 | tf_op jit(solution)/shard_map/ppermute | solution.py:38
  111.9 0.8 constant_dynamic-slice_fusion.2
  112.8 3.5 %all-to-all-start = ((f32[4,256,128]{2,0,1:T(4,128)}), f32[4,256,128]{2,0,1:T(4,128)S(1)}, u32[]{:S(2)}, u32[]{:S(2)}) async-start(f32[4,256,128]{2,0,1:T(4,128)} %constant_dynamic-slice_fusion.2), calls=%async_computation | async-start | bytes 1048576 | tf_op jit(solution)/shard_map/all_to_all | solution.py:42
  116.3 1.4 fusion.9
  118.0 10.6 %all-to-all-done = f32[4,256,128]{2,0,1:T(4,128)S(1)} async-done(((f32[4,256,128]{2,0,1:T(4,128)}), f32[4,256,128]{2,0,1:T(4,128)S(1)}, u32[]{:S(2)}, u32[]{:S(2)}) %all-to-all-start) | async-done | bytes 524320 | tf_op jit(solution)/shard_map/all_to_all | solution.py:42
  129.5 2.1 %all-gather.5.cloned.1.call-done = bf16[16,256,128]{2,1,0:T(8,128)(2,1)} async-done(((bf16[16,128,128]{2,1,0:T(8,128)(2,1)}), bf16[16,256,128]{2,1,0:T(8,128)(2,1)}) %all-gather.5.cloned.1.call-update) | async-done | bytes 1048592 | tf_op jit(solution)/shard_map/all_gather | solution.py:45
  131.6 36.5 %while.10 = (s32[]{:T(128)}, f32[16,128,4,32]{1,3,2,0:T(8,128)S(1)}, bf16[16,256,128]{2,1,0:T(8,128)(2,1)}, pred[256]{0:T(512)(128)(4,1)S(1)}, bf16[16,128,4,32]...) while((s32[]{:T(128)}, ...), condition=%wide.region_5.6_spmd, body=%wide.region_2.5_spmd.sunk | while | flops 59636736 | bytes 2861665 | solution.py:62
  131.6 0.9 constant_dynamic-slice_fusion.4
  133.3 0.5 fusion.48
  133.9 0.9 constant_dynamic-slice_fusion.4
  136.2 0.9 constant_dynamic-slice_fusion.4
  138.4 0.9 constant_dynamic-slice_fusion.4
  140.7 0.9 constant_dynamic-slice_fusion.4
  142.5 0.5 fusion.48
  143.0 0.9 constant_dynamic-slice_fusion.4
  145.3 0.9 constant_dynamic-slice_fusion.4
  147.0 0.5 fusion.48
  147.5 0.9 constant_dynamic-slice_fusion.4
  149.8 0.9 constant_dynamic-slice_fusion.4
  152.1 0.9 constant_dynamic-slice_fusion.4
  154.4 0.9 constant_dynamic-slice_fusion.4
  156.1 0.5 fusion.48
  156.7 0.9 constant_dynamic-slice_fusion.4
  158.9 0.9 constant_dynamic-slice_fusion.4
  161.2 0.9 constant_dynamic-slice_fusion.4
  163.5 0.9 constant_dynamic-slice_fusion.4
  165.8 0.9 constant_dynamic-slice_fusion.4
  168.4 3.3 %fusion.15 = f32[16,128,128]{2,1,0:T(8,128)} fusion(f32[16,128,128]{2,1,0:T(8,128)S(1)} %copy.18, f32[16,128,512]{2,1,0:T(8,128)} %get-tuple-element.78, f32[128]{0:T(128)S(1)} %copy-done.7, f32[128,128]{1,0:T(8,128)S(1)} %copy-done.5), kind=kOutput, calls=%fused_computation.25 | convolution fusion | flops 403963904 | bytes 3211776 | tf_op jit(solution)/shard_map/rjd,dc->rjc/dot_general | solution.py:64
  (151 shorter events, 21.7 us)
Async XLA Ops:
  6.5 3.5 %copy-start = (f32[128,512]{1,0:T(8,128)S(1)}, f32[128,512]{1,0:T(8,128)}, u32[]{:S(2)}) copy-start(f32[128,512]{1,0:T(8,128)} %param.14) | copy-start | bytes 786436
  6.5 122.9 %all-gather.3.cloned.1.call-start = ((), (), s32[]{:S(2)}) async-start(), calls=%async_computation.1 | async-start | bytes 1572864 | tf_op jit(solution)/shard_map/all_gather | solution.py:46
  10.1 8.2 %copy-start.1 = (f32[16,128,128]{2,1,0:T(8,128)S(1)}, f32[16,128,128]{2,1,0:T(8,128)}, u32[]{:S(2)}) copy-start(f32[16,128,128]{2,1,0:T(8,128)} %param.10) | copy-start | bytes 3145732
  10.1 8.2 %copy-start.2 = (f32[128]{0:T(128)S(1)}, f32[128]{0:T(128)}, u32[]{:S(2)}) copy-start(f32[128]{0:T(128)} %param.13) | copy-start | bytes 1540
  10.1 8.1 %copy-start.3 = (f32[128]{0:T(128)S(1)}, f32[128]{0:T(128)}, u32[]{:S(2)}) copy-start(f32[128]{0:T(128)} %param.12) | copy-start | bytes 1540
  10.1 8.1 %copy-start.4 = (f32[128,4]{0,1:T(4,128)S(1)}, f32[128,4]{0,1:T(4,128)}, u32[]{:S(2)}) copy-start(f32[128,4]{0,1:T(4,128)} %param.16) | copy-start | bytes 6148
  18.1 99.8 %copy-start.6 = (s32[256]{0:T(256)S(1)}, s32[256]{0:T(256)}, u32[]{:S(2)}) copy-start(s32[256]{0:T(256)} %param.11) | copy-start | bytes 3076
  18.2 113.4 %all-gather.5.cloned.1.call-start = ((), (), s32[]{:S(2)}) async-start(), calls=%async_computation.2 | async-start | bytes 1572864 | tf_op jit(solution)/shard_map/all_gather | solution.py:45
  19.9 7.1 %collective-permute-start = (f32[4,16,128]{2,0,1:T(4,128)S(1)}, f32[4,16,128]{2,0,1:T(4,128)S(1)}, u32[]{:S(2)}, u32[]{:S(2)}) collective-permute-start(f32[4,16,128]{2,0,1:T(4,128)S(1)} %convolution_bitcast_fusion.1), channel_id=1, source_target_pairs={{0,2},{2,4},{4,6},{6,8},{8,10},{10,12},{12,14},{14,16},{16,18},{18... | collective-permute-start | bytes 98312 | tf_op jit(solution)/shard_map/ppermute | solution.py:38
  26.9 6.0 %collective-permute-start.1 = (f32[4,16,128]{2,0,1:T(4,128)S(1)}, f32[4,16,128]{2,0,1:T(4,128)S(1)}, u32[]{:S(2)}, u32[]{:S(2)}) collective-permute-start(f32[4,16,128]{2,0,1:T(4,128)S(1)} %collective-permute-done), channel_id=1, source_target_pairs={{0,2},{2,4},{4,6},{6,8},{8,10},{10,12},{12,14},{14,16},{16,18},{18... | collective-permute-start | bytes 98312 | tf_op jit(solution)/shard_map/ppermute | solution.py:38
  33.0 6.0 %collective-permute-start.2 = (f32[4,16,128]{2,0,1:T(4,128)S(1)}, f32[4,16,128]{2,0,1:T(4,128)S(1)}, u32[]{:S(2)}, u32[]{:S(2)}) collective-permute-start(f32[4,16,128]{2,0,1:T(4,128)S(1)} %collective-permute-done.1), channel_id=1, source_target_pairs={{0,2},{2,4},{4,6},{6,8},{8,10},{10,12},{12,14},{14,16},{16,18},{18... | collective-permute-start | bytes 98312 | tf_op jit(solution)/shard_map/ppermute | solution.py:38
  39.0 6.0 %collective-permute-start.3 = (f32[4,16,128]{2,0,1:T(4,128)S(1)}, f32[4,16,128]{2,0,1:T(4,128)S(1)}, u32[]{:S(2)}, u32[]{:S(2)}) collective-permute-start(f32[4,16,128]{2,0,1:T(4,128)S(1)} %collective-permute-done.2), channel_id=1, source_target_pairs={{0,2},{2,4},{4,6},{6,8},{8,10},{10,12},{12,14},{14,16},{16,18},{18... | collective-permute-start | bytes 98312 | tf_op jit(solution)/shard_map/ppermute | solution.py:38
  45.1 6.0 %collective-permute-start.4 = (f32[4,16,128]{2,0,1:T(4,128)S(1)}, f32[4,16,128]{2,0,1:T(4,128)S(1)}, u32[]{:S(2)}, u32[]{:S(2)}) collective-permute-start(f32[4,16,128]{2,0,1:T(4,128)S(1)} %collective-permute-done.3), channel_id=1, source_target_pairs={{0,2},{2,4},{4,6},{6,8},{8,10},{10,12},{12,14},{14,16},{16,18},{18... | collective-permute-start | bytes 98312 | tf_op jit(solution)/shard_map/ppermute | solution.py:38
  51.1 6.0 %collective-permute-start.5 = (f32[4,16,128]{2,0,1:T(4,128)S(1)}, f32[4,16,128]{2,0,1:T(4,128)S(1)}, u32[]{:S(2)}, u32[]{:S(2)}) collective-permute-start(f32[4,16,128]{2,0,1:T(4,128)S(1)} %collective-permute-done.4), channel_id=1, source_target_pairs={{0,2},{2,4},{4,6},{6,8},{8,10},{10,12},{12,14},{14,16},{16,18},{18... | collective-permute-start | bytes 98312 | tf_op jit(solution)/shard_map/ppermute | solution.py:38
  57.1 6.0 %collective-permute-start.6 = (f32[4,16,128]{2,0,1:T(4,128)S(1)}, f32[4,16,128]{2,0,1:T(4,128)S(1)}, u32[]{:S(2)}, u32[]{:S(2)}) collective-permute-start(f32[4,16,128]{2,0,1:T(4,128)S(1)} %collective-permute-done.5), channel_id=1, source_target_pairs={{0,2},{2,4},{4,6},{6,8},{8,10},{10,12},{12,14},{14,16},{16,18},{18... | collective-permute-start | bytes 98312 | tf_op jit(solution)/shard_map/ppermute | solution.py:38
  63.2 6.0 %collective-permute-start.7 = (f32[4,16,128]{2,0,1:T(4,128)S(1)}, f32[4,16,128]{2,0,1:T(4,128)S(1)}, u32[]{:S(2)}, u32[]{:S(2)}) collective-permute-start(f32[4,16,128]{2,0,1:T(4,128)S(1)} %collective-permute-done.6), channel_id=1, source_target_pairs={{0,2},{2,4},{4,6},{6,8},{8,10},{10,12},{12,14},{14,16},{16,18},{18... | collective-permute-start | bytes 98312 | tf_op jit(solution)/shard_map/ppermute | solution.py:38
  69.2 6.0 %collective-permute-start.8 = (f32[4,16,128]{2,0,1:T(4,128)S(1)}, f32[4,16,128]{2,0,1:T(4,128)S(1)}, u32[]{:S(2)}, u32[]{:S(2)}) collective-permute-start(f32[4,16,128]{2,0,1:T(4,128)S(1)} %collective-permute-done.7), channel_id=1, source_target_pairs={{0,2},{2,4},{4,6},{6,8},{8,10},{10,12},{12,14},{14,16},{16,18},{18... | collective-permute-start | bytes 98312 | tf_op jit(solution)/shard_map/ppermute | solution.py:38
  75.2 6.0 %collective-permute-start.9 = (f32[4,16,128]{2,0,1:T(4,128)S(1)}, f32[4,16,128]{2,0,1:T(4,128)S(1)}, u32[]{:S(2)}, u32[]{:S(2)}) collective-permute-start(f32[4,16,128]{2,0,1:T(4,128)S(1)} %collective-permute-done.8), channel_id=1, source_target_pairs={{0,2},{2,4},{4,6},{6,8},{8,10},{10,12},{12,14},{14,16},{16,18},{18... | collective-permute-start | bytes 98312 | tf_op jit(solution)/shard_map/ppermute | solution.py:38
  81.3 6.0 %collective-permute-start.10 = (f32[4,16,128]{2,0,1:T(4,128)S(1)}, f32[4,16,128]{2,0,1:T(4,128)S(1)}, u32[]{:S(2)}, u32[]{:S(2)}) collective-permute-start(f32[4,16,128]{2,0,1:T(4,128)S(1)} %collective-permute-done.9), channel_id=1, source_target_pairs={{0,2},{2,4},{4,6},{6,8},{8,10},{10,12},{12,14},{14,16},{16,18},{18... | collective-permute-start | bytes 98312 | tf_op jit(solution)/shard_map/ppermute | solution.py:38
  87.3 6.0 %collective-permute-start.11 = (f32[4,16,128]{2,0,1:T(4,128)S(1)}, f32[4,16,128]{2,0,1:T(4,128)S(1)}, u32[]{:S(2)}, u32[]{:S(2)}) collective-permute-start(f32[4,16,128]{2,0,1:T(4,128)S(1)} %collective-permute-done.10), channel_id=1, source_target_pairs={{0,2},{2,4},{4,6},{6,8},{8,10},{10,12},{12,14},{14,16},{16,18},{18... | collective-permute-start | bytes 98312 | tf_op jit(solution)/shard_map/ppermute | solution.py:38
  93.4 6.0 %collective-permute-start.12 = (f32[4,16,128]{2,0,1:T(4,128)S(1)}, f32[4,16,128]{2,0,1:T(4,128)S(1)}, u32[]{:S(2)}, u32[]{:S(2)}) collective-permute-start(f32[4,16,128]{2,0,1:T(4,128)S(1)} %collective-permute-done.11), channel_id=1, source_target_pairs={{0,2},{2,4},{4,6},{6,8},{8,10},{10,12},{12,14},{14,16},{16,18},{18... | collective-permute-start | bytes 98312 | tf_op jit(solution)/shard_map/ppermute | solution.py:38
  99.4 6.0 %collective-permute-start.13 = (f32[4,16,128]{2,0,1:T(4,128)S(1)}, f32[4,16,128]{2,0,1:T(4,128)S(1)}, u32[]{:S(2)}, u32[]{:S(2)}) collective-permute-start(f32[4,16,128]{2,0,1:T(4,128)S(1)} %collective-permute-done.12), channel_id=1, source_target_pairs={{0,2},{2,4},{4,6},{6,8},{8,10},{10,12},{12,14},{14,16},{16,18},{18... | collective-permute-start | bytes 98312 | tf_op jit(solution)/shard_map/ppermute | solution.py:38
  105.4 6.0 %collective-permute-start.14 = (f32[4,16,128]{2,0,1:T(4,128)S(1)}, f32[4,16,128]{2,0,1:T(4,128)S(1)}, u32[]{:S(2)}, u32[]{:S(2)}) collective-permute-start(f32[4,16,128]{2,0,1:T(4,128)S(1)} %collective-permute-done.13), channel_id=1, source_target_pairs={{0,2},{2,4},{4,6},{6,8},{8,10},{10,12},{12,14},{14,16},{16,18},{18... | collective-permute-start | bytes 98312 | tf_op jit(solution)/shard_map/ppermute | solution.py:38
  112.8 15.8 %all-to-all-start = ((f32[4,256,128]{2,0,1:T(4,128)}), f32[4,256,128]{2,0,1:T(4,128)S(1)}, u32[]{:S(2)}, u32[]{:S(2)}) async-start(f32[4,256,128]{2,0,1:T(4,128)} %constant_dynamic-slice_fusion.2), calls=%async_computation | async-start | bytes 1048576 | tf_op jit(solution)/shard_map/all_to_all | solution.py:42
  131.6 36.8 %copy-start.5 = (f32[128,128]{1,0:T(8,128)S(1)}, f32[128,128]{1,0:T(8,128)}, u32[]{:S(2)}) copy-start(f32[128,128]{1,0:T(8,128)} %param.17) | copy-start | bytes 196612
  131.6 36.8 %copy-start.7 = (f32[128]{0:T(128)S(1)}, f32[128]{0:T(128)}, u32[]{:S(2)}) copy-start(f32[128]{0:T(128)} %param.15) | copy-start | bytes 1540
Sparse Core Ops, SparseCore 0:
  18.3 23.9 all-gather.2
  105.6 25.9 all-gather.4
